TPU v7x, 32 devices: a whole 2x2x4 slice. The times are simulated.
32 devices in a mesh: dp: 4 (over y, x), expert: 4 (over z), tensor: 2 (over core).
Axes of the slice: x: 2, y: 2, z: 4, core: 2. Of those that a mesh axis runs over, the one named last changes fastest.
Arguments:
- out_grad: bfloat16 [2048, 2048], P(('dp', 'expert'), 'tensor'), may hold values from -6 to 6
- seq_ids: int32 [16, 128], P(('dp', 'expert')), may hold values from 0 to 3, never falling along the last dimension, each value on 1 to 64 neighbouring positions
- seq_weights: float32 [16, 4], P(('dp', 'expert')), may hold values from -1.5 to 1.5
- expert_ids: int32 [2048, 2], P(('dp', 'expert')), may hold values from 0 to 3, all different within a row; in each aligned block of 128 rows (0 to 127, 128 to 255, ...) at most 96 rows name the same one
- route_probs: bfloat16 [2048, 2], P(('dp', 'expert')), may hold values from 0.19921875 to 1
- down_weight: bfloat16 [4, 7168, 2048], P('expert', ('dp', 'tensor')), may hold values from -0.0625 to 0.0625
- gate_pre: bfloat16 [4, 7168, 1536], P('expert', ('dp', 'tensor')), may hold values from -6 to 6
- up_pre: bfloat16 [4, 7168, 1536], P('expert', ('dp', 'tensor')), may hold values from -6 to 6
Outputs:
- grad_gate: bfloat16 [4, 7168, 1536], P('expert', ('dp', 'tensor'))
- grad_up: bfloat16 [4, 7168, 1536], P('expert', ('dp', 'tensor'))
- grad_down: bfloat16 [4, 7168, 2048], P('expert', ('dp', 'tensor'))
- grad_probs: float32 [2048, 2], P(('dp', 'expert'))
Inputs may be any that keep to these rules, and one draw needn't show every extreme that they name: `expert_ids`: the two experts of a token differ. Among the 128 tokens of one shard no expert is named more than 96 times, and in every draw some expert is named exactly 96 times by the tokens of some shard. `seq_ids`: along a shard's row the ids never fall; each of the 4 ids names 1 to 64 tokens of the row, and one names exactly 64.
All inputs are finite; a program needn't handle non-finite values.
Results may differ from a plain program's by a relative error of at most 0.0064.
Values may be sent and summed in bfloat16 or wider, within the bound.
A program may use at most 128 MiB of HBM per device.

v0:
```python
import jax
import jax.numpy as jnp
from jax import lax
from jax.sharding import PartitionSpec as P


def silu_parts(pre_act):
    logistic = jax.nn.sigmoid(pre_act)
    return (pre_act * logistic, logistic * (1.0 + pre_act * (1.0 - logistic)))


def local(out_grad, seq_ids, seq_weights, expert_ids, route_probs, down_weight, gate_pre, up_pre):
    experts = lax.axis_size("expert")
    columns = lax.axis_size("dp")
    token_count = seq_ids.shape[1]
    capacity = gate_pre.shape[2] // (columns * experts)
    half_width = out_grad.shape[1]
    seq_count = seq_weights.shape[1]
    block_size = experts * capacity
    gate_local = gate_pre[0]
    up_local = up_pre[0]
    weight_local = down_weight[0]
    member = (seq_ids[0][:, None] == jnp.arange(seq_count, dtype=jnp.int32)[None, :]).astype(
        jnp.float32
    )
    weight_tok = jnp.sum(member * seq_weights[0][None, :], axis=1)
    scaled = (weight_tok[:, None] * out_grad.astype(jnp.float32)).astype(jnp.bfloat16)
    chosen = expert_ids.reshape(-1)
    onehot = (chosen[:, None] == jnp.arange(experts, dtype=jnp.int32)[None, :]).astype(jnp.int32)
    earlier = jnp.cumsum(onehot, axis=0) - onehot
    slot_index = chosen * capacity + jnp.sum(earlier * onehot, axis=1)
    send_rows = (
        jnp.zeros((block_size, half_width), jnp.bfloat16)
        .at[slot_index]
        .set(jnp.repeat(scaled, 2, axis=0))
    )
    send_probs = jnp.zeros((block_size,), jnp.bfloat16).at[slot_index].set(route_probs.reshape(-1))
    copies = jnp.tile(send_rows, (columns, 1))
    copy_probs = jnp.tile(send_probs, (columns,))
    arrived, arrived_probs = (
        lax.all_to_all(copies, ("dp", "expert"), split_axis=0, concat_axis=0, tiled=True),
        lax.all_to_all(copy_probs, ("dp", "expert"), split_axis=0, concat_axis=0, tiled=True),
    )
    gathered = lax.all_gather(arrived, "tensor", axis=1, tiled=True)
    gate_piece = gate_local.astype(jnp.float32)
    up_piece = up_local.astype(jnp.float32)
    activated, derivative = silu_parts(gate_piece)
    hidden = (activated * up_piece).astype(jnp.bfloat16)
    upstream = lax.dot_general(
        weight_local, gathered, (((1,), (1,)), ((), ())), preferred_element_type=jnp.float32
    )
    partial_value = jnp.sum(upstream * hidden.astype(jnp.float32), axis=0)
    grad_hidden = arrived_probs.astype(jnp.float32)[None, :] * upstream
    gate_out = (grad_hidden * up_piece * derivative).astype(jnp.bfloat16)
    up_out = (grad_hidden * activated).astype(jnp.bfloat16)
    weighted = (arrived_probs.astype(jnp.float32)[:, None] * gathered.astype(jnp.float32)).astype(
        jnp.bfloat16
    )
    grad_w = jnp.dot(hidden, weighted, preferred_element_type=jnp.float32)
    gate_acc = gate_out
    up_acc = up_out
    probe = partial_value
    grad_w, gate_acc, up_acc, probe = (grad_w, gate_acc, up_acc, probe)
    summed = lax.psum(probe, ("dp", "tensor"))
    own_totals = lax.dynamic_slice_in_dim(summed, lax.axis_index("dp") * block_size, block_size, 0)
    returned = lax.all_to_all(own_totals, "expert", split_axis=0, concat_axis=0, tiled=True)
    grad_probs = returned[slot_index].reshape(token_count, 2)
    return (gate_acc[None], up_acc[None], grad_w.astype(jnp.bfloat16)[None], grad_probs)


def solution(mesh):
    return jax.shard_map(
        local,
        mesh=mesh,
        in_specs=(
            P(("dp", "expert"), "tensor"),
            P(("dp", "expert"), None),
            P(("dp", "expert"), None),
            P(("dp", "expert"), None),
            P(("dp", "expert"), None),
            P("expert", ("dp", "tensor"), None),
            P("expert", ("dp", "tensor"), None),
            P("expert", ("dp", "tensor"), None),
        ),
        out_specs=(
            P("expert", ("dp", "tensor"), None),
            P("expert", ("dp", "tensor"), None),
            P("expert", ("dp", "tensor"), None),
            P(("dp", "expert"), None),
        ),
        check_vma=False,
    )
```

profile of v0, /device:TPU:0, one launch (start us, length us, event | category | flops | bytes accessed | tf_op | source)
XLA Modules:
  0.0 166.8 jit_solution(17966599329222551912)
XLA Ops:
  7.2 0.8 copy.39
  8.0 0.1 eq.44
  8.1 0.1 eq.40
  8.3 0.7 broadcast_multiply_fusion
  9.0 1.2 reduce-window.6
  10.3 0.1 copy.41
  10.6 0.1 copy.38
  10.7 0.1 mul.82
  10.8 0.8 select_reduce_fusion
  11.6 1.1 multiply_convert_fusion.5
  12.6 0.3 broadcast_in_dim.28
  12.9 0.2 reshape.128
  13.2 1.9 %scatter_custom_fusion.1 = bf16[384,1024]{1,0:T(8,128)(2,1)S(1)} fusion(s32[256]{0:T(256)S(1)} %bitcast.78, bf16[256,1024]{1,0:T(8,128)(2,1)S(1)} %reshape.128, bf16[]{:T(256)} %constant.8.clone.1), kind=kCustom, calls=%fused_computation.29 | custom fusion | bytes 786434 | tf_op jit(solution)/shard_map/scatter | solution.py:35
  15.1 0.4 tile.21
  15.5 80.9 %all_to_all.30 = bf16[16,96,1024]{2,1,0:T(8,128)(2,1)} all-to-all(bf16[16,96,1024]{2,1,0:T(8,128)(2,1)S(1)} %bitcast.76), channel_id=1, replica_groups=mesh['dp'=4,'expert'=4,'tensor'=2] {'dp','expert'}, dimensions={0} | all-to-all | bytes 6291456 | tf_op jit(solution)/shard_map/all_to_all | solution.py:41
  96.4 0.1 copy.43
  96.6 0.1 reshape.120
  96.7 2.2 %scatter_custom_fusion = bf16[384]{0:T(512)(128)(2,1)S(1)} fusion(s32[256]{0:T(256)S(1)} %bitcast.79, bf16[256]{0:T(256)(128)(2,1)S(1)} %reshape.120, bf16[]{:T(256)} %constant.8.clone.1), kind=kCustom, calls=%fused_computation.44 | custom fusion | bytes 770 | tf_op jit(solution)/shard_map/scatter | solution.py:37
  99.0 0.6 copy.44
  99.6 3.5 %all-to-all-start = ((bf16[16,96,1]{1,2,0:T(2,128)(2,1)}), bf16[16,96,1]{1,2,0:T(2,128)(2,1)S(1)}, u32[]{:S(2)}, u32[]{:S(2)}) async-start(bf16[16,96,1]{1,2,0:T(2,128)(2,1)} %copy.44), calls=%async_computation | async-start | bytes 16384 | tf_op jit(solution)/shard_map/all_to_all | solution.py:42
  103.1 7.2 %all-to-all-done = bf16[16,96,1]{1,2,0:T(2,128)(2,1)S(1)} async-done(((bf16[16,96,1]{1,2,0:T(2,128)(2,1)}), bf16[16,96,1]{1,2,0:T(2,128)(2,1)S(1)}, u32[]{:S(2)}, u32[]{:S(2)}) %all-to-all-start) | async-done | bytes 3104 | tf_op jit(solution)/shard_map/all_to_all | solution.py:42
  110.4 0.2 all-gather.2.cloned.1.call-done
  110.6 14.0 %fusion.10 = (f32[1536]{0:T(1024)S(1)}, bf16[1,896,1536]{2,1,0:T(8,128)(2,1)}, bf16[1,896,1536]{2,1,0:T(8,128)(2,1)}) fusion(bf16[1,896,1536]{2,1,0:T(8,128)(2,1)S(1)} %copy-done.1, bf16[1,896,1536]{2,1,0:T(8,128)(2,1)} %param.14, f32[1536]{0:T(1024)S(1)} %reshape.105, bf16[1536,2048]{1,0:T(8,128)(2,1)} %all-gather.2.cloned.1.call-done, ...), kind=kOutput, calls=%fused_computation.21 | convolution fusion | flops 5666044416 | bytes 20983808 | tf_op jit(solution)/shard_map/dot_general | solution.py:49
  124.5 14.6 %psum.7 = f32[1536]{0:T(1024)S(1)} all-reduce(f32[1536]{0:T(1024)S(1)} %get-tuple-element.20), channel_id=1, replica_groups=mesh['dp'=4,'expert'=4,'tensor'=2] {'dp','tensor'}, use_global_device_ids=true, to_apply=%region_7.8 | all-reduce | flops 1536 | bytes 12288 | tf_op jit(solution)/shard_map/psum | solution.py:64
  139.2 0.7 all_to_all.24
  139.9 4.6 %all-to-all-start.2 = ((f32[4,96,1]{1,2,0:T(1,128)}), f32[4,96,1]{1,2,0:T(1,128)S(1)}, u32[]{:S(2)}, u32[]{:S(2)}) async-start(f32[4,96,1]{1,2,0:T(1,128)} %bitcast.18), calls=%async_computation.2 | async-start | bytes 4096 | tf_op jit(solution)/shard_map/all_to_all | solution.py:66
  144.5 11.4 %convert_bitcast_fusion = bf16[1,896,2048]{2,1,0:T(8,128)(2,1)} fusion(bf16[1536,2048]{1,0:T(8,128)(2,1)} %all-gather.2.cloned.1.call-done, f32[1536]{0:T(1024)S(1)} %reshape.105, bf16[1,896,1536]{2,1,0:T(8,128)(2,1)S(1)} %copy-done.1, bf16[1,896,1536]{2,1,0:T(8,128)(2,1)} %param.14), kind=kOutput, calls=%fused_computation.25 | convolution fusion | flops 5659426816 | bytes 15472640 | tf_op jit(solution)/shard_map/dot_general | solution.py:59
  155.9 0.5 broadcast.90
  156.4 0.7 reduce.7
  157.2 1.9 %gather_fusion = f32[256]{0:T(256)S(1)} fusion(f32[384]{0:T(512)S(1)} %all_to_all.26, s32[1024]{0:T(1024)S(1)} %pad_clamp_fusion), kind=kCustom, calls=%fused_computation | custom fusion | bytes 3072 | tf_op jit(solution)/shard_map/gather | solution.py:67
  159.1 0.1 reshape.104
  159.3 0.6 copy.46
  (22 shorter events, 0.8 us)
Async XLA Ops:
  7.2 103.4 %all-gather.2.cloned.1.call-start = ((), (), s32[]{:S(2)}) async-start(), calls=%async_computation.3 | async-start | bytes 9437184 | tf_op jit(solution)/shard_map/all_gather | solution.py:44
  15.5 80.9 %copy-start = (bf16[128,2]{0,1:T(2,128)(2,1)S(1)}, bf16[128,2]{0,1:T(2,128)(2,1)}, u32[]{:S(2)}) copy-start(bf16[128,2]{0,1:T(2,128)(2,1)} %param.12) | copy-start | bytes 1540
  15.5 95.1 %copy-start.1 = (bf16[1,896,1536]{2,1,0:T(8,128)(2,1)S(1)}, bf16[1,896,1536]{2,1,0:T(8,128)(2,1)}, u32[]{:S(2)}) copy-start(bf16[1,896,1536]{2,1,0:T(8,128)(2,1)} %param.15) | copy-start | bytes 8257540
  99.6 10.7 %all-to-all-start = ((bf16[16,96,1]{1,2,0:T(2,128)(2,1)}), bf16[16,96,1]{1,2,0:T(2,128)(2,1)S(1)}, u32[]{:S(2)}, u32[]{:S(2)}) async-start(bf16[16,96,1]{1,2,0:T(2,128)(2,1)} %copy.44), calls=%async_computation | async-start | bytes 16384 | tf_op jit(solution)/shard_map/all_to_all | solution.py:42
  139.9 16.0 %all-to-all-start.2 = ((f32[4,96,1]{1,2,0:T(1,128)}), f32[4,96,1]{1,2,0:T(1,128)S(1)}, u32[]{:S(2)}, u32[]{:S(2)}) async-start(f32[4,96,1]{1,2,0:T(1,128)} %bitcast.18), calls=%async_computation.2 | async-start | bytes 4096 | tf_op jit(solution)/shard_map/all_to_all | solution.py:66
Sparse Core Ops, SparseCore 0:
  96.5 13.9 all-gather.1
where the time goes:
time: 167 us
  blocking collectives  95.4 us (57%)
  matrix products  25.4 us (15%)
  between operations  14.2 us (9%)
  local copies, waits for them, and re-layouts  11.7 us (7%)
  starting transfers between devices  8.11 us (5%)
  waiting for transfers between devices  7.37 us (4%)
  other arithmetic  4.55 us (3%)
    all_to_all x1, blocking collectives, local(): lax.all_to_all(copies, ('dp', 'expert'), split_axis=0, concat_axis=0, til...  80.9 us
    psum x1, blocking collectives, local(): summed = lax.psum(probe, ('dp', 'tensor'))  14.6 us
    dot_general x1, matrix products, local(): lax.dot_general(weight_local, gathered, (((1,), (1,)), ((), ())), preferr...  14 us
    dot_general x1, matrix products, local(): grad_w = jnp.dot(hidden, weighted, preferred_element_type=jnp.float32)  11.4 us
    all_to_all x1, waiting for transfers between devices, local(): lax.all_to_all(copy_probs, ('dp', 'expert'), split_axis=0, concat_axis=0,...  7.16 us
    all_to_all x1, starting transfers between devices, local(): lax.all_to_all(own_totals, 'expert', split_axis=0, concat_axis=0, tiled=T...  4.59 us
    all_to_all x1, starting transfers between devices, local(): lax.all_to_all(copy_probs, ('dp', 'expert'), split_axis=0, concat_axis=0,...  3.48 us
  transfers between devices with their start and end apart: 3, of which 2 were waited for; matrix products, arithmetic and copies ran while one was open for 9% of the time, Pallas kernels for 0%

commit v1 on v0

--- a/solution.py
+++ b/solution.py
@@ -61,7 +61,7 @@
     up_acc = up_out
     probe = partial_value
     grad_w, gate_acc, up_acc, probe = (grad_w, gate_acc, up_acc, probe)
-    summed = lax.psum(probe, ("dp", "tensor"))
+    summed = jnp.sum(lax.all_gather(probe, ("dp", "tensor")), axis=0)
     own_totals = lax.dynamic_slice_in_dim(summed, lax.axis_index("dp") * block_size, block_size, 0)
     returned = lax.all_to_all(own_totals, "expert", split_axis=0, concat_axis=0, tiled=True)
     grad_probs = returned[slot_index].reshape(token_count, 2)

time: 167 us -> 162 us (0.970)
  blocking collectives: 95.4 us -> 90.3 us
    psum x1 -> x0, blocking collectives: 14.6 us -> none  [local(): summed = lax.psum(probe, ('dp', 'tensor'))]
    all_gather x0 -> x1, blocking collectives: none -> 9.41 us  [local(): summed = jnp.sum(lax.all_gather(probe, ('dp', 'tensor')), axis=0)]
where the time goes in v1:
time: 162 us
  blocking collectives  90.3 us (56%)
  matrix products  25.4 us (16%)
  between operations  14.2 us (9%)
  local copies, waits for them, and re-layouts  11.7 us (7%)
  starting transfers between devices  8.12 us (5%)
  waiting for transfers between devices  7.37 us (5%)
  other arithmetic  4.59 us (3%)
    all_to_all x1, blocking collectives, local(): lax.all_to_all(copies, ('dp', 'expert'), split_axis=0, concat_axis=0, til...  80.9 us
    dot_general x1, matrix products, local(): lax.dot_general(weight_local, gathered, (((1,), (1,)), ((), ())), preferr...  14 us
    dot_general x1, matrix products, local(): grad_w = jnp.dot(hidden, weighted, preferred_element_type=jnp.float32)  11.4 us
    all_gather x1, blocking collectives, local(): summed = jnp.sum(lax.all_gather(probe, ('dp', 'tensor')), axis=0)  9.41 us
    all_to_all x1, waiting for transfers between devices, local(): lax.all_to_all(copy_probs, ('dp', 'expert'), split_axis=0, concat_axis=0,...  7.16 us
    all_to_all x1, starting transfers between devices, local(): lax.all_to_all(own_totals, 'expert', split_axis=0, concat_axis=0, tiled=T...  4.61 us
    all_to_all x1, starting transfers between devices, local(): lax.all_to_all(copy_probs, ('dp', 'expert'), split_axis=0, concat_axis=0,...  3.48 us
  transfers between devices with their start and end apart: 3, of which 2 were waited for; matrix products, arithmetic and copies ran while one was open for 9% of the time, Pallas kernels for 0%

profile of v1, /device:TPU:0, one launch (start us, length us, event | category | flops | bytes accessed | tf_op | source)
XLA Modules:
  0.0 161.7 jit_solution(16693667524796966703)
XLA Ops:
  7.2 0.8 copy.39
  8.0 0.1 eq.44
  8.1 0.1 eq.40
  8.3 0.7 broadcast_multiply_fusion
  9.0 1.2 reduce-window.6
  10.3 0.1 copy.41
  10.6 0.1 copy.38
  10.7 0.1 mul.82
  10.8 0.8 select_reduce_fusion
  11.6 1.1 multiply_convert_fusion.5
  12.6 0.3 broadcast_in_dim.28
  12.9 0.2 reshape.128
  13.2 1.9 %scatter_custom_fusion.1 = bf16[384,1024]{1,0:T(8,128)(2,1)S(1)} fusion(s32[256]{0:T(256)S(1)} %bitcast.78, bf16[256,1024]{1,0:T(8,128)(2,1)S(1)} %reshape.128, bf16[]{:T(256)} %constant.8.clone.1), kind=kCustom, calls=%fused_computation.29 | custom fusion | bytes 786434 | tf_op jit(solution)/shard_map/scatter | solution.py:35
  15.1 0.4 tile.21
  15.5 80.9 %all_to_all.30 = bf16[16,96,1024]{2,1,0:T(8,128)(2,1)} all-to-all(bf16[16,96,1024]{2,1,0:T(8,128)(2,1)S(1)} %bitcast.76), channel_id=1, replica_groups=mesh['dp'=4,'expert'=4,'tensor'=2] {'dp','expert'}, dimensions={0} | all-to-all | bytes 6291456 | tf_op jit(solution)/shard_map/all_to_all | solution.py:41
  96.4 0.1 copy.43
  96.6 0.1 reshape.120
  96.7 2.2 %scatter_custom_fusion = bf16[384]{0:T(512)(128)(2,1)S(1)} fusion(s32[256]{0:T(256)S(1)} %bitcast.79, bf16[256]{0:T(256)(128)(2,1)S(1)} %reshape.120, bf16[]{:T(256)} %constant.8.clone.1), kind=kCustom, calls=%fused_computation.44 | custom fusion | bytes 770 | tf_op jit(solution)/shard_map/scatter | solution.py:37
  99.0 0.6 copy.44
  99.6 3.5 %all-to-all-start = ((bf16[16,96,1]{1,2,0:T(2,128)(2,1)}), bf16[16,96,1]{1,2,0:T(2,128)(2,1)S(1)}, u32[]{:S(2)}, u32[]{:S(2)}) async-start(bf16[16,96,1]{1,2,0:T(2,128)(2,1)} %copy.44), calls=%async_computation | async-start | bytes 16384 | tf_op jit(solution)/shard_map/all_to_all | solution.py:42
  103.1 7.2 %all-to-all-done = bf16[16,96,1]{1,2,0:T(2,128)(2,1)S(1)} async-done(((bf16[16,96,1]{1,2,0:T(2,128)(2,1)}), bf16[16,96,1]{1,2,0:T(2,128)(2,1)S(1)}, u32[]{:S(2)}, u32[]{:S(2)}) %all-to-all-start) | async-done | bytes 3104 | tf_op jit(solution)/shard_map/all_to_all | solution.py:42
  110.4 0.2 all-gather.4.cloned.1.call-done
  110.6 14.0 %fusion.10 = (f32[1536]{0:T(1024)S(1)}, bf16[1,896,1536]{2,1,0:T(8,128)(2,1)}, bf16[1,896,1536]{2,1,0:T(8,128)(2,1)}) fusion(bf16[1,896,1536]{2,1,0:T(8,128)(2,1)S(1)} %copy-done.1, bf16[1,896,1536]{2,1,0:T(8,128)(2,1)} %param.14, f32[1536]{0:T(1024)S(1)} %reshape.105, bf16[1536,2048]{1,0:T(8,128)(2,1)} %all-gather.4.cloned.1.call-done, ...), kind=kOutput, calls=%fused_computation.21 | convolution fusion | flops 5666044416 | bytes 20983808 | tf_op jit(solution)/shard_map/dot_general | solution.py:49
  124.5 9.4 %all-gather.1 = f32[8,1,1536]{2,1,0:T(1,128)S(1)} all-gather(f32[1,1,1536]{2,1,0:T(1,128)S(1)} %reshape.133), channel_id=2, replica_groups=mesh['dp'=4,'expert'=4,'tensor'=2] {'dp','tensor'}, dimensions={0}, use_global_device_ids=true | all-gather | bytes 55296 | tf_op jit(solution)/shard_map/all_gather | solution.py:64
  134.1 0.7 all_to_all.24
  134.8 4.6 %all-to-all-start.2 = ((f32[4,96,1]{1,2,0:T(1,128)}), f32[4,96,1]{1,2,0:T(1,128)S(1)}, u32[]{:S(2)}, u32[]{:S(2)}) async-start(f32[4,96,1]{1,2,0:T(1,128)} %bitcast.18), calls=%async_computation.2 | async-start | bytes 4096 | tf_op jit(solution)/shard_map/all_to_all | solution.py:66
  139.4 11.4 %convert_bitcast_fusion = bf16[1,896,2048]{2,1,0:T(8,128)(2,1)} fusion(bf16[1536,2048]{1,0:T(8,128)(2,1)} %all-gather.4.cloned.1.call-done, f32[1536]{0:T(1024)S(1)} %reshape.105, bf16[1,896,1536]{2,1,0:T(8,128)(2,1)S(1)} %copy-done.1, bf16[1,896,1536]{2,1,0:T(8,128)(2,1)} %param.14), kind=kOutput, calls=%fused_computation.25 | convolution fusion | flops 5659426816 | bytes 15472640 | tf_op jit(solution)/shard_map/dot_general | solution.py:59
  150.8 0.5 broadcast.90
  151.3 0.7 reduce.8
  152.1 1.9 %gather_fusion = f32[256]{0:T(256)S(1)} fusion(f32[384]{0:T(512)S(1)} %all_to_all.26, s32[1024]{0:T(1024)S(1)} %pad_clamp_fusion), kind=kCustom, calls=%fused_computation | custom fusion | bytes 3072 | tf_op jit(solution)/shard_map/gather | solution.py:67
  154.0 0.1 reshape.104
  154.2 0.6 copy.46
  (24 shorter events, 0.8 us)
Async XLA Ops:
  7.2 103.4 %all-gather.4.cloned.1.call-start = ((), (), s32[]{:S(2)}) async-start(), calls=%async_computation.3 | async-start | bytes 9437184 | tf_op jit(solution)/shard_map/all_gather | solution.py:44
  15.5 80.9 %copy-start = (bf16[128,2]{0,1:T(2,128)(2,1)S(1)}, bf16[128,2]{0,1:T(2,128)(2,1)}, u32[]{:S(2)}) copy-start(bf16[128,2]{0,1:T(2,128)(2,1)} %param.12) | copy-start | bytes 1540
  15.5 95.1 %copy-start.1 = (bf16[1,896,1536]{2,1,0:T(8,128)(2,1)S(1)}, bf16[1,896,1536]{2,1,0:T(8,128)(2,1)}, u32[]{:S(2)}) copy-start(bf16[1,896,1536]{2,1,0:T(8,128)(2,1)} %param.15) | copy-start | bytes 8257540
  99.6 10.7 %all-to-all-start = ((bf16[16,96,1]{1,2,0:T(2,128)(2,1)}), bf16[16,96,1]{1,2,0:T(2,128)(2,1)S(1)}, u32[]{:S(2)}, u32[]{:S(2)}) async-start(bf16[16,96,1]{1,2,0:T(2,128)(2,1)} %copy.44), calls=%async_computation | async-start | bytes 16384 | tf_op jit(solution)/shard_map/all_to_all | solution.py:42
  134.8 16.0 %all-to-all-start.2 = ((f32[4,96,1]{1,2,0:T(1,128)}), f32[4,96,1]{1,2,0:T(1,128)S(1)}, u32[]{:S(2)}, u32[]{:S(2)}) async-start(f32[4,96,1]{1,2,0:T(1,128)} %bitcast.18), calls=%async_computation.2 | async-start | bytes 4096 | tf_op jit(solution)/shard_map/all_to_all | solution.py:66
Sparse Core Ops, SparseCore 0:
  96.5 13.9 all-gather.3
